TPU v7x, 128 devices: a whole 4x4x4 slice. The times are simulated.
128 devices in a mesh: owner: 4 (over y_lo, core), rows: 32 (over z, y_hi, x).
Axes of the slice: x: 4, y: 4 (y_hi: 2, y_lo: 2; y = y_hi * 2 + y_lo), z: 4, core: 2. Of those that a mesh axis runs over, the one named last changes fastest.
Arguments:
- train_gate: float32 [128, 2048, 768], P('owner', 'rows'), may hold values from -0.125 to 0.125
- train_up: float32 [128, 2048, 768], P('owner', 'rows'), may hold values from -0.125 to 0.125
- router_weight: float32 [2048, 128], P('rows', 'owner'), may hold values from -0.125 to 0.125
- router_gain: float32 [2048], P('rows'), may hold values from 0.25 to 1.75
Outputs:
- ready_gate: bfloat16 [128, 768, 2048], P(('owner', 'rows'))
- ready_up: bfloat16 [128, 768, 2048], P(('owner', 'rows'))
- serve_router: bfloat16 [2048, 128], replicated
All inputs are finite; a program needn't handle non-finite values.
Results may differ from a plain program's by a relative error of at most 0.001.
Values may be sent and summed in bfloat16 or wider, within the bound.
No kernel may reach another device: no remote copies, remote signals or barrier semaphores. Data moves between devices by JAX's collectives and lax.ppermute only.
A program may use at most 128 MiB of HBM per device.

v0:
```python
import jax
import jax.numpy as jnp
from jax import lax
from jax.sharding import PartitionSpec as P


def copy_for_each(array, axis):
    devices = lax.axis_size(axis)
    return lax.all_to_all(
        jnp.broadcast_to(array[None], (devices, *array.shape)), axis, 0, 0, tiled=True
    )


def in_order(pieces, dim):
    pieces = jnp.moveaxis(pieces, 0, dim)
    lengths = pieces.shape
    return pieces.reshape(*lengths[:dim], lengths[dim] * lengths[dim + 1], *lengths[dim + 2 :])


def collect(array, axis, dim):
    pieces = copy_for_each(array, axis)
    return in_order(pieces, dim)


def on_device(train_gate, train_up, router_weight, router_gain):
    narrow_gate, narrow_up = (train_gate.astype(jnp.bfloat16), train_up.astype(jnp.bfloat16))
    ready_gate, ready_up = (
        lax.all_to_all(narrow_gate, "rows", split_axis=0, concat_axis=1, tiled=True),
        lax.all_to_all(narrow_up, "rows", split_axis=0, concat_axis=1, tiled=True),
    )
    ready_gate = jnp.transpose(ready_gate, (0, 2, 1))
    ready_up = jnp.transpose(ready_up, (0, 2, 1))
    part_router = (router_weight * router_gain[:, None]).astype(jnp.bfloat16)
    row_router = collect(part_router, "rows", 0)
    serve_router = collect(row_router, "owner", 1)
    return (ready_gate, ready_up, serve_router)


def solution(mesh):
    placed = (P("owner", "rows", None), P("owner", "rows", None), P("rows", "owner"), P("rows"))
    return jax.shard_map(
        on_device,
        mesh=mesh,
        in_specs=placed,
        out_specs=(P(("owner", "rows"), None, None), P(("owner", "rows"), None, None), P()),
        check_vma=False,
    )
```

profile of v0, /device:TPU:2, one launch (start us, length us, event | category | flops | bytes accessed | tf_op | source)
XLA Modules:
  0.0 140.7 jit_solution(14053241097780356728)
XLA Ops:
  0.6 0.7 multiply_convert_fusion
  1.4 0.2 reshape.19
  1.6 19.9 %all_to_all.34 = bf16[32,2,1024]{2,1,0:T(2,128)(2,1)S(1)} all-to-all(bf16[32,2,1024]{2,1,0:T(2,128)(2,1)S(1)} %reshape.19), channel_id=1, replica_groups=mesh['owner'=4,'rows'=32] {'rows'}, dimensions={0} | all-to-all | bytes 262144 | tf_op jit(solution)/shard_map/all_to_all | solution.py:9
  21.5 0.2 reshape.20
  21.7 0.1 copy.16
  21.9 0.3 broadcast_in_dim.7
  22.1 0.9 broadcast_in_dim.16
  23.0 3.5 %all-to-all-start.3 = ((bf16[4,2048,32]{1,2,0:T(8,128)(2,1)}), bf16[4,2048,32]{1,2,0:T(8,128)(2,1)S(1)}, u32[]{:S(2)}, u32[]{:S(2)}) async-start(bf16[4,2048,32]{1,2,0:T(8,128)(2,1)} %broadcast_in_dim.16), calls=%async_computation.3 | async-start | bytes 1048576 | tf_op jit(solution)/shard_map/all_to_all | solution.py:9
  26.5 4.9 %convert_element_type.9 = bf16[32,64,768]{2,1,0:T(8,128)(2,1)} convert(f32[32,64,768]{2,1,0:T(8,128)} %param.4) | non-fusion elementwise | flops 1572864 | bytes 9437184 | tf_op jit(solution)/shard_map/convert_element_type | solution.py:26
  31.4 3.9 %all-to-all-done.3 = bf16[4,2048,32]{1,2,0:T(8,128)(2,1)S(1)} async-done(((bf16[4,2048,32]{1,2,0:T(8,128)(2,1)}), bf16[4,2048,32]{1,2,0:T(8,128)(2,1)S(1)}, u32[]{:S(2)}, u32[]{:S(2)}) %all-to-all-start.3) | async-done | bytes 524320 | tf_op jit(solution)/shard_map/all_to_all | solution.py:9
  35.2 0.0 copy-start
  35.2 0.8 copy-done
  36.0 5.2 %all-to-all-start = ((bf16[32,64,768]{2,1,0:T(8,128)(2,1)}), bf16[32,64,768]{2,1,0:T(8,128)(2,1)S(1)}, u32[]{:S(2)}, u32[]{:S(2)}) async-start(bf16[32,64,768]{2,1,0:T(8,128)(2,1)} %convert_element_type.9), calls=%async_computation | async-start | bytes 6291456 | tf_op jit(solution)/shard_map/all_to_all | solution.py:28
  41.2 4.9 %convert_element_type.10 = bf16[32,64,768]{2,1,0:T(8,128)(2,1)} convert(f32[32,64,768]{2,1,0:T(8,128)} %param.5) | non-fusion elementwise | flops 1572864 | bytes 9437184 | tf_op jit(solution)/shard_map/convert_element_type | solution.py:26
  46.1 38.4 %all-to-all-done = bf16[32,64,768]{2,1,0:T(8,128)(2,1)S(1)} async-done(((bf16[32,64,768]{2,1,0:T(8,128)(2,1)}), bf16[32,64,768]{2,1,0:T(8,128)(2,1)S(1)}, u32[]{:S(2)}, u32[]{:S(2)}) %all-to-all-start) | async-done | bytes 3145760 | tf_op jit(solution)/shard_map/all_to_all | solution.py:28
  84.5 6.8 %all-to-all-start.1 = ((bf16[32,64,768]{2,1,0:T(8,128)(2,1)}), bf16[32,64,768]{2,1,0:T(8,128)(2,1)}, u32[]{:S(2)}, u32[]{:S(2)}) async-start(bf16[32,64,768]{2,1,0:T(8,128)(2,1)} %convert_element_type.10), calls=%async_computation.1 | async-start | bytes 6291456 | tf_op jit(solution)/shard_map/all_to_all | solution.py:29
  91.3 2.0 %copy.19 = bf16[2048,128]{1,0:T(8,128)(2,1)} copy(bf16[2048,128]{0,1:T(8,128)(2,1)} %bitcast.15) | data formatting | bytes 1048576
  93.3 2.9 %copy.17 = bf16[1,768,2048]{2,1,0:T(8,128)(2,1)} copy(bf16[1,768,2048]{1,2,0:T(8,128)(2,1)S(1)} %bitcast.14) | data formatting | bytes 6291456
  96.2 39.8 %all-to-all-done.1 = bf16[32,64,768]{2,1,0:T(8,128)(2,1)} async-done(((bf16[32,64,768]{2,1,0:T(8,128)(2,1)}), bf16[32,64,768]{2,1,0:T(8,128)(2,1)}, u32[]{:S(2)}, u32[]{:S(2)}) %all-to-all-start.1) | async-done | bytes 3145760 | tf_op jit(solution)/shard_map/all_to_all | solution.py:29
  136.0 4.6 %copy.18 = bf16[1,768,2048]{2,1,0:T(8,128)(2,1)} copy(bf16[1,768,2048]{1,2,0:T(8,128)(2,1)} %bitcast.3) | data formatting | bytes 6291456
  (1 shorter events, 0.0 us)
Async XLA Ops:
  23.0 12.3 %all-to-all-start.3 = ((bf16[4,2048,32]{1,2,0:T(8,128)(2,1)}), bf16[4,2048,32]{1,2,0:T(8,128)(2,1)S(1)}, u32[]{:S(2)}, u32[]{:S(2)}) async-start(bf16[4,2048,32]{1,2,0:T(8,128)(2,1)} %broadcast_in_dim.16), calls=%async_computation.3 | async-start | bytes 1048576 | tf_op jit(solution)/shard_map/all_to_all | solution.py:9
  35.2 0.8 copy-start
  36.0 48.5 %all-to-all-start = ((bf16[32,64,768]{2,1,0:T(8,128)(2,1)}), bf16[32,64,768]{2,1,0:T(8,128)(2,1)S(1)}, u32[]{:S(2)}, u32[]{:S(2)}) async-start(bf16[32,64,768]{2,1,0:T(8,128)(2,1)} %convert_element_type.9), calls=%async_computation | async-start | bytes 6291456 | tf_op jit(solution)/shard_map/all_to_all | solution.py:28
  84.5 51.5 %all-to-all-start.1 = ((bf16[32,64,768]{2,1,0:T(8,128)(2,1)}), bf16[32,64,768]{2,1,0:T(8,128)(2,1)}, u32[]{:S(2)}, u32[]{:S(2)}) async-start(bf16[32,64,768]{2,1,0:T(8,128)(2,1)} %convert_element_type.10), calls=%async_computation.1 | async-start | bytes 6291456 | tf_op jit(solution)/shard_map/all_to_all | solution.py:29
where the time goes:
time: 141 us
  waiting for transfers between devices  82.1 us (58%)
  blocking collectives  19.9 us (14%)
  starting transfers between devices  15.4 us (11%)
  local copies, waits for them, and re-layouts  12 us (9%)
  other arithmetic  10.5 us (7%)
    all_to_all x1, waiting for transfers between devices, on_device(): lax.all_to_all(narrow_up, 'rows', split_axis=0, concat_axis=1, tiled=True)  39.8 us
    all_to_all x1, waiting for transfers between devices, on_device(): lax.all_to_all(narrow_gate, 'rows', split_axis=0, concat_axis=1, tiled=True)  38.4 us
    all_to_all x1, blocking collectives, copy_for_each(): lax.all_to_all(jnp.broadcast_to(array[None], (devices, *array.shape)), ax...  19.9 us
    unnamed x8, local copies, waits for them, and re-layouts  10.8 us
    all_to_all x1, starting transfers between devices, on_device(): lax.all_to_all(narrow_up, 'rows', split_axis=0, concat_axis=1, tiled=True)  6.76 us
    all_to_all x1, starting transfers between devices, on_device(): lax.all_to_all(narrow_gate, 'rows', split_axis=0, concat_axis=1, tiled=True)  5.17 us
    convert_element_type x1, other arithmetic, on_device(): train_up.astype(jnp.bfloat16)  4.92 us
    convert_element_type x1, other arithmetic, on_device(): train_gate.astype(jnp.bfloat16)  4.9 us
  transfers between devices with their start and end apart: 3, of which 3 were waited for; matrix products, arithmetic and copies ran while one was open for 10% of the time, Pallas kernels for 0%

commit v1 on v0

v1 whole, which is shorter than its diff:
```python
import jax
import jax.numpy as jnp
from jax import lax
from jax.sharding import PartitionSpec as P


def on_device(train_gate, train_up, router_weight, router_gain):
    narrow_gate, narrow_up = (train_gate.astype(jnp.bfloat16), train_up.astype(jnp.bfloat16))
    ready_gate, ready_up = (
        lax.all_to_all(narrow_gate, "rows", split_axis=0, concat_axis=1, tiled=True),
        lax.all_to_all(narrow_up, "rows", split_axis=0, concat_axis=1, tiled=True),
    )
    ready_gate = jnp.transpose(ready_gate, (0, 2, 1))
    ready_up = jnp.transpose(ready_up, (0, 2, 1))
    part_router = (router_weight * router_gain[:, None]).astype(jnp.bfloat16)
    row_router = lax.all_gather(part_router, "rows", axis=0, tiled=True)
    serve_router = lax.all_gather(row_router, "owner", axis=1, tiled=True)
    return (ready_gate, ready_up, serve_router)


def solution(mesh):
    placed = (P("owner", "rows", None), P("owner", "rows", None), P("rows", "owner"), P("rows"))
    return jax.shard_map(
        on_device,
        mesh=mesh,
        in_specs=placed,
        out_specs=(P(("owner", "rows"), None, None), P(("owner", "rows"), None, None), P()),
        check_vma=False,
    )
```

time: 141 us -> 208 us (1.48)
  the two profiles are of different devices: /device:TPU:2 before, /device:TPU:1 now
where the time goes in v1:
time: 208 us; the launch traced here: 207 us
  blocking collectives  131 us (63%)
  waiting for transfers between devices  35.5 us (17%)
  starting transfers between devices  20.6 us (10%)
  local copies, waits for them, and re-layouts  9.9 us (5%)
  other arithmetic  9.81 us (5%)
    all_gather x1, blocking collectives, on_device(): row_router = lax.all_gather(part_router, 'rows', axis=0, tiled=True)  109 us
    all_to_all x1, waiting for transfers between devices, on_device(): lax.all_to_all(narrow_gate, 'rows', split_axis=0, concat_axis=1, tiled=True)  35.5 us
    all_gather x1, blocking collectives, on_device(): serve_router = lax.all_gather(row_router, 'owner', axis=1, tiled=True)  21.2 us
    all_to_all x1, starting transfers between devices, on_device(): lax.all_to_all(narrow_gate, 'rows', split_axis=0, concat_axis=1, tiled=True)  11.3 us
    unnamed x8, local copies, waits for them, and re-layouts  9.8 us
    all_to_all x1, starting transfers between devices, on_device(): lax.all_to_all(narrow_up, 'rows', split_axis=0, concat_axis=1, tiled=True)  9.28 us
    convert_element_type x1, other arithmetic, on_device(): train_up.astype(jnp.bfloat16)  4.91 us
    convert_element_type x1, other arithmetic, on_device(): train_gate.astype(jnp.bfloat16)  4.9 us
  transfers between devices with their start and end apart: 2, of which 1 were waited for; matrix products, arithmetic and copies ran while one was open for 5% of the time, Pallas kernels for 0%

profile of v1, /device:TPU:1, one launch (start us, length us, event | category | flops | bytes accessed | tf_op | source)
XLA Modules:
  0.0 207.1 jit_solution(5680264515938017051)
XLA Ops:
  0.6 4.9 %convert_element_type.9 = bf16[32,64,768]{2,1,0:T(8,128)(2,1)} convert(f32[32,64,768]{2,1,0:T(8,128)} %param.4) | non-fusion elementwise | flops 1572864 | bytes 9437184 | tf_op jit(solution)/shard_map/convert_element_type | solution.py:8
  5.5 11.3 %all-to-all-start = ((bf16[32,64,768]{2,1,0:T(8,128)(2,1)}), bf16[32,64,768]{2,1,0:T(8,128)(2,1)S(1)}, u32[]{:S(2)}, u32[]{:S(2)}) async-start(bf16[32,64,768]{2,1,0:T(8,128)(2,1)} %convert_element_type.9), calls=%async_computation | async-start | bytes 6291456 | tf_op jit(solution)/shard_map/all_to_all | solution.py:10
  16.9 4.9 %convert_element_type.10 = bf16[32,64,768]{2,1,0:T(8,128)(2,1)} convert(f32[32,64,768]{2,1,0:T(8,128)} %param.5) | non-fusion elementwise | flops 1572864 | bytes 9437184 | tf_op jit(solution)/shard_map/convert_element_type | solution.py:8
  21.8 0.0 copy-start
  21.8 0.0 copy-start.1
  21.8 35.5 %all-to-all-done = bf16[32,64,768]{2,1,0:T(8,128)(2,1)S(1)} async-done(((bf16[32,64,768]{2,1,0:T(8,128)(2,1)}), bf16[32,64,768]{2,1,0:T(8,128)(2,1)S(1)}, u32[]{:S(2)}, u32[]{:S(2)}) %all-to-all-start) | async-done | bytes 3145760 | tf_op jit(solution)/shard_map/all_to_all | solution.py:10
  57.3 9.3 %all-to-all-start.1 = ((bf16[32,64,768]{2,1,0:T(8,128)(2,1)}), bf16[32,64,768]{2,1,0:T(8,128)(2,1)}, u32[]{:S(2)}, u32[]{:S(2)}) async-start(bf16[32,64,768]{2,1,0:T(8,128)(2,1)} %convert_element_type.10), calls=%async_computation.1 | async-start | bytes 6291456 | tf_op jit(solution)/shard_map/all_to_all | solution.py:11
  66.6 0.0 copy-done
  66.6 0.0 copy-done.1
  66.6 109.3 %all-gather = bf16[32,64,32]{1,2,0:T(8,128)(2,1)S(1)} all-gather(bf16[1,64,32]{1,2,0:T(8,128)(2,1)S(1)} %fusion), channel_id=1, replica_groups=mesh['owner'=4,'rows'=32] {'rows'}, dimensions={0}, use_global_device_ids=true | all-gather | bytes 135168 | tf_op jit(solution)/shard_map/all_gather | solution.py:16
  175.9 0.1 copy.16
  176.0 0.3 reshape.14
  176.3 21.2 %all_gather.7 = bf16[2048,128]{0,1:T(8,128)(2,1)} all-gather(bf16[2048,32]{0,1:T(8,128)(2,1)S(1)} %reshape.14), channel_id=1, replica_groups=mesh['owner'=4,'rows'=32] {'owner'}, dimensions={1}, use_global_device_ids=true | all-gather | bytes 655360 | tf_op jit(solution)/shard_map/all_gather | solution.py:17
  197.5 2.0 copy.19
  199.6 2.9 %copy.17 = bf16[1,768,2048]{2,1,0:T(8,128)(2,1)} copy(bf16[1,768,2048]{1,2,0:T(8,128)(2,1)S(1)} %bitcast.10) | data formatting | bytes 6291456
  202.4 0.0 all-to-all-done.1
  202.4 4.6 %copy.18 = bf16[1,768,2048]{2,1,0:T(8,128)(2,1)} copy(bf16[1,768,2048]{1,2,0:T(8,128)(2,1)} %bitcast.3) | data formatting | bytes 6291456
  (1 shorter events, 0.0 us)
Async XLA Ops:
  5.5 51.7 %all-to-all-start = ((bf16[32,64,768]{2,1,0:T(8,128)(2,1)}), bf16[32,64,768]{2,1,0:T(8,128)(2,1)S(1)}, u32[]{:S(2)}, u32[]{:S(2)}) async-start(bf16[32,64,768]{2,1,0:T(8,128)(2,1)} %convert_element_type.9), calls=%async_computation | async-start | bytes 6291456 | tf_op jit(solution)/shard_map/all_to_all | solution.py:10
  21.8 44.8 %copy-start = (f32[64,32]{0,1:T(8,128)S(1)}, f32[64,32]{0,1:T(8,128)}, u32[]{:S(2)}) copy-start(f32[64,32]{0,1:T(8,128)} %param.6) | copy-start | bytes 24580
  21.8 44.8 %copy-start.1 = (f32[64]{0:T(128)S(1)}, f32[64]{0:T(128)}, u32[]{:S(2)}) copy-start(f32[64]{0:T(128)} %param.7) | copy-start | bytes 772
  57.3 145.2 %all-to-all-start.1 = ((bf16[32,64,768]{2,1,0:T(8,128)(2,1)}), bf16[32,64,768]{2,1,0:T(8,128)(2,1)}, u32[]{:S(2)}, u32[]{:S(2)}) async-start(bf16[32,64,768]{2,1,0:T(8,128)(2,1)} %convert_element_type.10), calls=%async_computation.1 | async-start | bytes 6291456 | tf_op jit(solution)/shard_map/all_to_all | solution.py:11

commit v2 on v1

v2 whole, which is shorter than its diff:
```python
import jax
import jax.numpy as jnp
from jax import lax
from jax.experimental import pallas as pl
from jax.experimental.pallas import tpu as pltpu
from jax.sharding import PartitionSpec as P

AXES = ("owner", "rows")
LANES = 128
WHOLE = pl.BlockSpec(memory_space=pltpu.VMEM)
COST = pl.CostEstimate(flops=100_000_000, bytes_accessed=20_000_000, transcendentals=0)


def places():
    for owner in range(4):
        for row in range(32):
            yield {"z": row // 8, "yh": row // 4 % 2, "x": row % 4, "yl": owner // 2, "core": owner % 2}


def place(at):
    return (at["yl"] * 2 + at["core"]) * 32 + at["z"] * 8 + at["yh"] * 4 + at["x"]


def swap(block, axis):
    pairs = [(place(at), place(dict(at, **{axis: at[axis] ^ 1}))) for at in places()]
    return lax.ppermute(block, AXES, pairs)


def pack_kernel(gate_ref, up_ref, out_ref, held, sems):
    deep, wide = gate_ref.shape[1:]
    step, batches = held.shape[2], held.shape[1]
    tiles = wide // LANES

    def copy(which, ref, batch):
        return pltpu.make_async_copy(
            ref.at[pl.ds(batch * step, step)], held.at[which, batch], sems.at[which, batch]
        )

    for batch in range(batches):
        for which, ref in enumerate((gate_ref, up_ref)):
            copy(which, ref, batch).start()

    def convert(batch, carry):
        for which, ref in enumerate((gate_ref, up_ref)):
            copy(which, ref, batch).wait()
            for tile in range(tiles):
                out_ref[pl.ds(batch * step, step), pl.ds((which * tiles + tile) * deep, deep), :] = held[
                    which, batch, :, :, tile * LANES : (tile + 1) * LANES
                ].astype(jnp.bfloat16)
        return carry

    lax.fori_loop(0, batches, convert, 0)


def pack(gate, up, extra):
    pieces, deep, wide = gate.shape
    step = 2
    total = 2 * deep * wide // LANES + extra
    anywhere = pl.BlockSpec(memory_space=pltpu.HBM)
    return pl.pallas_call(
        pack_kernel,
        in_specs=[anywhere, anywhere],
        out_specs=WHOLE,
        out_shape=pltpu.VMEM((pieces, total, LANES), jnp.bfloat16),
        scratch_shapes=[
            pltpu.VMEM((2, pieces // step, step, deep, wide), jnp.float32),
            pltpu.SemaphoreType.DMA((2, pieces // step)),
        ],
        compiler_params=pltpu.CompilerParams(vmem_limit_bytes=44 * 1024 * 1024),
        cost_estimate=COST,
        name="pack",
    )(gate, up)


def stamp_kernel(payload_ref, mine_ref, other_ref, out_ref):
    del payload_ref
    upper = lax.axis_index("owner") // 2 == 1
    mine, other = mine_ref[...].astype(jnp.float32), other_ref[...].astype(jnp.float32)
    both = jnp.concatenate([jnp.where(upper, other, mine), jnp.where(upper, mine, other)], axis=0).T
    deep = both.shape[0]
    block = jnp.concatenate([both[: deep // 2], both[deep // 2 :]], axis=1).astype(jnp.bfloat16)
    first = out_ref.shape[1] - deep // 2
    for piece in range(out_ref.shape[0]):
        out_ref[piece, first:, :] = block


def stamp(payload, mine, other):
    return pl.pallas_call(
        stamp_kernel,
        in_specs=[WHOLE, WHOLE, WHOLE],
        out_specs=WHOLE,
        out_shape=jax.ShapeDtypeStruct(payload.shape, payload.dtype),
        input_output_aliases={0: 0},
        compiler_params=pltpu.CompilerParams(vmem_limit_bytes=16 * 1024 * 1024),
        name="stamp",
    )(payload, mine, other)


def unpack_kernel(source, gate_ref, up_ref):
    pieces = source.shape[0]
    deep = gate_ref.shape[1] // pieces
    tiles = pl.num_programs(0)
    pair = LANES // deep
    for which, out in enumerate((gate_ref, up_ref)):
        start = (which * tiles + pl.program_id(0)) * deep
        for i in range(pieces // pair):
            block = source[pl.ds(i * pair, pair), pl.ds(pl.multiple_of(start, deep), deep), :]
            out[:, i * LANES : (i + 1) * LANES] = block.reshape(LANES, LANES).T


def unpack(received, deep, wide):
    pieces = received.shape[0]
    out = pl.BlockSpec((LANES, pieces * deep), lambda j: (j, 0))
    shape = jax.ShapeDtypeStruct((wide, pieces * deep), jnp.bfloat16)
    return pl.pallas_call(
        unpack_kernel,
        grid=(wide // LANES,),
        in_specs=[WHOLE],
        out_specs=[out, out],
        out_shape=[shape, shape],
        compiler_params=pltpu.CompilerParams(vmem_limit_bytes=16 * 1024 * 1024),
        cost_estimate=COST,
        name="unpack",
    )(received)


def finish_kernel(mine_ref, other_ref, out_ref):
    pieces, half, lanes = mine_ref.shape
    upper = lax.axis_index("owner") % 2 == 1
    mine = mine_ref[...].reshape(pieces * half, lanes).astype(jnp.float32)
    other = other_ref[...].reshape(pieces * half, lanes).astype(jnp.float32)
    first, second = jnp.where(upper, other, mine), jnp.where(upper, mine, other)
    quarter = lanes // 4
    group = lax.broadcasted_iota(jnp.int32, first.shape, 1) // quarter
    for h in range(2):
        parts = [
            pltpu.roll(first, (lanes - 2 * quarter * h) % lanes, 1),
            pltpu.roll(second, (lanes + quarter - 2 * quarter * h) % lanes, 1),
            pltpu.roll(first, (lanes + quarter - 2 * quarter * h) % lanes, 1),
            pltpu.roll(second, (lanes + 2 * quarter - 2 * quarter * h) % lanes, 1),
        ]
        block = parts[3]
        for i in range(3):
            block = jnp.where(group == i, parts[i], block)
        out_ref[:, h * half : (h + 1) * half, :] = block.astype(jnp.bfloat16).reshape(pieces, half, lanes)


def finish(mine, other):
    pieces, half, lanes = mine.shape
    return pl.pallas_call(
        finish_kernel,
        in_specs=[WHOLE, WHOLE],
        out_specs=WHOLE,
        out_shape=jax.ShapeDtypeStruct((pieces, 2 * half, lanes), jnp.bfloat16),
        compiler_params=pltpu.CompilerParams(vmem_limit_bytes=8 * 1024 * 1024),
        name="finish",
    )(mine, other)


def on_device(train_gate, train_up, router_weight, router_gain):
    pieces, deep, wide = train_gate.shape
    part = (router_weight.T * router_gain[None, :]).astype(jnp.bfloat16)
    part = lax.optimization_barrier(part)
    other_part = swap(part, "yl")
    payload = pack(train_gate, train_up, deep // 2)
    body = payload.shape[1] - deep // 2
    payload = stamp(payload, part, other_part)
    received = lax.all_to_all(payload, "rows", split_axis=0, concat_axis=0, tiled=True)
    mine = received[:, body:, :]
    other = swap(mine, "core")
    ready_gate, ready_up = unpack(received, deep, wide)
    serve_router = finish(mine, other).reshape(pieces * deep, LANES)
    return (ready_gate[None], ready_up[None], serve_router)


def solution(mesh):
    placed = (P("owner", "rows", None), P("owner", "rows", None), P("rows", "owner"), P("rows"))
    return jax.shard_map(
        on_device,
        mesh=mesh,
        in_specs=placed,
        out_specs=(P(("owner", "rows"), None, None), P(("owner", "rows"), None, None), P()),
        check_vma=False,
    )
```

time: 208 us -> 103 us (0.50)
  blocking collectives: 131 us -> 86.3 us
  waiting for transfers between devices: 35.5 us -> 0.01 us
  starting transfers between devices: 20.6 us -> 4.95 us
  Pallas kernels: 0 us -> 10.2 us
  local copies, waits for them, and re-layouts: 9.9 us -> 0.02 us
  other arithmetic: 9.81 us -> 0.72 us
    all_gather x2 -> x0, blocking collectives: 131 us -> none  [the longest x1 109 us: on_device(): row_router = lax.all_gather(part_router, 'rows', axis=0, tiled=True)]
    all_to_all x0 -> x1, blocking collectives: none -> 86.3 us  [on_device(): lax.all_to_all(payload, 'rows', split_axis=0, concat_axis=0, tiled=True)]
    all_to_all x2 -> x0, waiting for transfers between devices: 35.5 us -> none  [the longest x1 35.5 us: on_device(): lax.all_to_all(narrow_gate, 'rows', split_axis=0, concat_axis=1, tiled=True)]
    all_to_all x2 -> x0, starting transfers between devices: 20.6 us -> none  [the longest x1 11.3 us: on_device(): lax.all_to_all(narrow_gate, 'rows', split_axis=0, concat_axis=1, tiled=True)]
    pallas_call x0 -> x4, Pallas kernels: none -> 10.2 us  [the longest x1 4.86 us: pack(): pl.pallas_call(pack_kernel, in_specs=[anywhere, anywhere], out_specs=WHOL...]
    unnamed x8 -> x0, local copies, waits for them, and re-layouts: 9.8 us -> none
    convert_element_type x2 -> x1, other arithmetic: 9.81 us -> 0.72 us  [on_device(): part = (router_weight.T * router_gain[None, :]).astype(jnp.bfloat16)]
    ppermute x0 -> x2, starting transfers between devices: none -> 4.95 us  [swap(): return lax.ppermute(block, AXES, pairs)]
  transfers between devices with their start and end apart: 2 -> 2, of which waited for: 1 -> 0; matrix products, arithmetic and copies ran while one was open for 5% -> 0% of each run, Pallas kernels for 0% -> 8%
where the time goes in v2:
time: 103 us
  blocking collectives  86.3 us (84%)
  Pallas kernels  10.2 us (10%)
  starting transfers between devices  4.95 us (5%)
    all_to_all x1, blocking collectives, on_device(): lax.all_to_all(payload, 'rows', split_axis=0, concat_axis=0, tiled=True)  86.3 us
    ppermute x2, starting transfers between devices, swap(): return lax.ppermute(block, AXES, pairs)  4.95 us
    pallas_call x1, Pallas kernels, pack(): pl.pallas_call(pack_kernel, in_specs=[anywhere, anywhere], out_specs=WHOL...  4.86 us
    pallas_call x1, Pallas kernels, unpack(): pl.pallas_call(unpack_kernel, grid=(wide // LANES,), in_specs=[WHOLE], ou...  3.79 us
  transfers between devices with their start and end apart: 2, of which 0 were waited for; matrix products, arithmetic and copies ran while one was open for 0% of the time, Pallas kernels for 8%

profile of v2, /device:TPU:1, one launch (start us, length us, event | category | flops | bytes accessed | tf_op | source)
XLA Modules:
  0.0 102.9 jit_solution(12395665656956698455)
XLA Ops:
  0.6 0.7 fusion.mine_ref
  1.4 2.1 %collective-permute-start = (bf16[32,64]{1,0:T(8,128)(2,1)S(1)}, bf16[32,64]{1,0:T(8,128)(2,1)S(1)}, u32[]{:S(2)}, u32[]{:S(2)}) collective-permute-start(bf16[32,64]{1,0:T(8,128)(2,1)S(1)} %fusion.mine_ref), channel_id=1, source_target_pairs={{0,64},{1,65},{2,66},{3,67},{4,68},{5,69},{6,70},{7,71},{8,72},{9,... | collective-permute-start | bytes 12296 | tf_op jit(solution)/shard_map/ppermute | solution.py:26
  3.5 4.9 %pack.1.payload_ref = bf16[32,800,128]{2,1,0:T(8,128)(2,1)S(1)} custom-call(f32[32,64,768]{2,1,0:T(8,128)} %gate_ref.1, f32[32,64,768]{2,1,0:T(8,128)} %up_ref.1), custom_call_target="tpu_custom_call" | custom-call | flops 100000000 | bytes 20000000 | tf_op jit(solution)/shard_map/pack/pallas_call | solution.py:60
  8.3 0.0 collective-permute-done.other_ref
  8.3 0.2 stamp.1
  8.5 86.3 %all_to_all.5.source = bf16[32,800,128]{2,1,0:T(8,128)(2,1)S(1)} all-to-all(bf16[32,800,128]{2,1,0:T(8,128)(2,1)S(1)} %stamp.1), channel_id=1, replica_groups=mesh['owner'=4,'rows'=32] {'rows'}, dimensions={0} | all-to-all | bytes 13107200 | tf_op jit(solution)/shard_map/all_to_all | solution.py:168
  94.9 2.8 %collective-permute-start.1 = (bf16[32,32,128]{2,1,0:T(8,128)(2,1)S(1)}, bf16[32,32,128]{2,1,0:T(8,128)(2,1)S(1)}, u32[]{:S(2)}, u32[]{:S(2)}) collective-permute-start(bf16[32,32,128]{2,1,0:T(8,128)(2,1)S(1)} %slice.4.mine_ref), channel_id=1, source_target_pairs={{0,32},{1,33},{2,34},{3,35},{4,36},{5,37},{6,38},{7,39},{8,40},{9,... | collective-permute-start | bytes 786440 | tf_op jit(solution)/shard_map/ppermute | solution.py:26
  97.7 3.8 %unpack.1 = (bf16[768,2048]{1,0:T(8,128)(2,1)}, bf16[768,2048]{1,0:T(8,128)(2,1)}) custom-call(bf16[32,800,128]{2,1,0:T(8,128)(2,1)S(1)} %all_to_all.5.source), custom_call_target="tpu_custom_call" | custom-call | flops 100000000 | bytes 20000000 | tf_op jit(solution)/shard_map/unpack/pallas_call | solution.py:115
  101.5 0.0 collective-permute-done.1.other_ref
  101.5 1.4 %finish.1 = bf16[32,64,128]{2,1,0:T(8,128)(2,1)} custom-call(bf16[32,32,128]{2,1,0:T(8,128)(2,1)S(1)} %slice.4.mine_ref, bf16[32,32,128]{2,1,0:T(8,128)(2,1)S(1)} %collective-permute-done.1.other_ref), custom_call_target="tpu_custom_call" | custom-call | tf_op jit(solution)/shard_map/finish/pallas_call | solution.py:150
  (1 shorter events, 0.0 us)
Async XLA Ops:
  1.4 7.0 %collective-permute-start = (bf16[32,64]{1,0:T(8,128)(2,1)S(1)}, bf16[32,64]{1,0:T(8,128)(2,1)S(1)}, u32[]{:S(2)}, u32[]{:S(2)}) collective-permute-start(bf16[32,64]{1,0:T(8,128)(2,1)S(1)} %fusion.mine_ref), channel_id=1, source_target_pairs={{0,64},{1,65},{2,66},{3,67},{4,68},{5,69},{6,70},{7,71},{8,72},{9,... | collective-permute-start | bytes 12296 | tf_op jit(solution)/shard_map/ppermute | solution.py:26
  94.9 6.6 %collective-permute-start.1 = (bf16[32,32,128]{2,1,0:T(8,128)(2,1)S(1)}, bf16[32,32,128]{2,1,0:T(8,128)(2,1)S(1)}, u32[]{:S(2)}, u32[]{:S(2)}) collective-permute-start(bf16[32,32,128]{2,1,0:T(8,128)(2,1)S(1)} %slice.4.mine_ref), channel_id=1, source_target_pairs={{0,32},{1,33},{2,34},{3,35},{4,36},{5,37},{6,38},{7,39},{8,40},{9,... | collective-permute-start | bytes 786440 | tf_op jit(solution)/shard_map/ppermute | solution.py:26

commit v3 on v2

v3 whole, which is shorter than its diff:
```python
import jax
import jax.numpy as jnp
from jax import lax
from jax.experimental import pallas as pl
from jax.experimental.pallas import tpu as pltpu
from jax.sharding import PartitionSpec as P

AXES = ("owner", "rows")
LANES = 128
WHOLE = pl.BlockSpec(memory_space=pltpu.VMEM)
COST = pl.CostEstimate(flops=100_000_000, bytes_accessed=20_000_000, transcendentals=0)


def places():
    for owner in range(4):
        for row in range(32):
            yield {"z": row // 8, "yh": row // 4 % 2, "x": row % 4, "yl": owner // 2, "core": owner % 2}


def place(at):
    return (at["yl"] * 2 + at["core"]) * 32 + at["z"] * 8 + at["yh"] * 4 + at["x"]


def swap(block, axis):
    pairs = [(place(at), place(dict(at, **{axis: at[axis] ^ 1}))) for at in places()]
    return lax.ppermute(block, AXES, pairs)


def pack_kernel(gate_ref, up_ref, out_ref, held, sems):
    batches, step, deep, wide = held.shape[1:]
    tiles = wide // LANES

    def copy(which, batch):
        source = (gate_ref, up_ref)[which]
        return pltpu.make_async_copy(source.at[pl.ds(batch * step, step)], held.at[which, batch], sems.at[which, batch])

    for batch in range(batches):
        for which in range(2):
            copy(which, batch).start()

    @pl.loop(0, batches)
    def _(batch):
        for which in range(2):
            copy(which, batch).wait()
            for tile in range(tiles):
                out_ref[pl.ds(batch * step, step), pl.ds((which * tiles + tile) * deep, deep), :] = held[
                    which, batch, :, :, tile * LANES : (tile + 1) * LANES
                ].astype(jnp.bfloat16)


def pack(gate, up, extra):
    pieces, deep, wide = gate.shape
    step = 4
    total = 2 * deep * wide // LANES + extra
    there = pl.BlockSpec(memory_space=pltpu.HBM)
    return pl.pallas_call(
        pack_kernel,
        in_specs=[there, there],
        out_specs=WHOLE,
        out_shape=pltpu.VMEM((pieces, total, LANES), jnp.bfloat16),
        scratch_shapes=[
            pltpu.VMEM((2, pieces // step, step, deep, wide), jnp.float32),
            pltpu.SemaphoreType.DMA((2, pieces // step)),
        ],
        compiler_params=pltpu.CompilerParams(vmem_limit_bytes=44 * 1024 * 1024),
        cost_estimate=COST,
        name="pack",
    )(gate, up)


def stamp_kernel(payload_ref, mine_ref, other_ref, gain_ref, out_ref):
    del payload_ref
    upper = lax.axis_index("owner") // 2 == 1
    mine, other = mine_ref[...] * gain_ref[...], other_ref[...] * gain_ref[...]
    both = jnp.concatenate([jnp.where(upper, other, mine), jnp.where(upper, mine, other)], axis=0).T
    half, width = both.shape[0] // 2, both.shape[1] // 2
    parts = [both[h * half : (h + 1) * half, w * width : (w + 1) * width] for w in range(2) for h in range(2)]
    swapped = jnp.concatenate([parts[i ^ 1] for i in range(4)], axis=1)
    block = jnp.where(lax.axis_index("owner") % 2 == 1, swapped, jnp.concatenate(parts, axis=1))
    block = block.astype(jnp.bfloat16)
    first = out_ref.shape[1] - half
    for piece in range(out_ref.shape[0]):
        out_ref[piece, first:, :] = block


def stamp(payload, mine, other, gain):
    return pl.pallas_call(
        stamp_kernel,
        in_specs=[WHOLE] * 4,
        out_specs=WHOLE,
        out_shape=jax.ShapeDtypeStruct(payload.shape, payload.dtype),
        input_output_aliases={0: 0},
        compiler_params=pltpu.CompilerParams(vmem_limit_bytes=16 * 1024 * 1024),
        name="stamp",
    )(payload, mine, other, gain)


def unpack_kernel(source, gate_ref, up_ref, held, sems):
    pieces = source.shape[0]
    deep = gate_ref.shape[1] // pieces
    tiles = held.shape[1]
    pair = LANES // deep

    def copy(which, tile):
        out = (gate_ref, up_ref)[which]
        return pltpu.make_async_copy(held.at[which, tile], out.at[pl.ds(tile * LANES, LANES)], sems.at[which, tile])

    @pl.loop(0, tiles)
    def _(tile):
        for which in range(2):
            start = pl.multiple_of((which * tiles + tile) * deep, deep)
            for i in range(pieces // pair):
                block = source[pl.ds(i * pair, pair), pl.ds(start, deep), :]
                held[which, tile, :, i * LANES : (i + 1) * LANES] = block.reshape(LANES, LANES).T
            copy(which, tile).start()

    @pl.loop(0, tiles)
    def _(tile):
        for which in range(2):
            copy(which, tile).wait()


def unpack(received, deep, wide):
    pieces = received.shape[0]
    there = pl.BlockSpec(memory_space=pltpu.HBM)
    shape = jax.ShapeDtypeStruct((wide, pieces * deep), jnp.bfloat16)
    return pl.pallas_call(
        unpack_kernel,
        in_specs=[WHOLE],
        out_specs=[there, there],
        out_shape=[shape, shape],
        scratch_shapes=[
            pltpu.VMEM((2, wide // LANES, LANES, pieces * deep), jnp.bfloat16),
            pltpu.SemaphoreType.DMA((2, wide // LANES)),
        ],
        compiler_params=pltpu.CompilerParams(vmem_limit_bytes=24 * 1024 * 1024),
        cost_estimate=COST,
        name="unpack",
    )(received)


def finish_kernel(mine_ref, other_ref, out_ref):
    pieces, half, lanes = mine_ref.shape
    upper = lax.axis_index("owner") % 2
    mine = mine_ref[...].reshape(pieces * half, lanes).astype(jnp.float32)
    other = other_ref[...].reshape(pieces * half, lanes).astype(jnp.float32)
    quarter = lanes // 4
    odd = lax.broadcasted_iota(jnp.int32, mine.shape, 1) // quarter % 2
    own = odd == upper
    crossed = jnp.where(own, other, mine)
    crossed = jnp.where(odd == 1, pltpu.roll(crossed, quarter, 1), pltpu.roll(crossed, lanes - quarter, 1))
    for h, block in enumerate((jnp.where(own, mine, other), crossed)):
        out_ref[:, h * half : (h + 1) * half, :] = block.astype(jnp.bfloat16).reshape(pieces, half, lanes)


def finish(mine, other):
    pieces, half, lanes = mine.shape
    return pl.pallas_call(
        finish_kernel,
        in_specs=[WHOLE, WHOLE],
        out_specs=WHOLE,
        out_shape=jax.ShapeDtypeStruct((pieces, 2 * half, lanes), jnp.bfloat16),
        compiler_params=pltpu.CompilerParams(vmem_limit_bytes=8 * 1024 * 1024),
        name="finish",
    )(mine, other)


def on_device(train_gate, train_up, router_weight, router_gain):
    pieces, deep, wide = train_gate.shape
    part = router_weight.T
    other_part = swap(part, "yl")
    payload = pack(train_gate, train_up, deep // 2)
    body = payload.shape[1] - deep // 2
    payload = stamp(payload, part, other_part, router_gain[None, :])
    received = lax.all_to_all(payload, "rows", split_axis=0, concat_axis=0, tiled=True)
    mine = received[:, body:, :]
    other = swap(mine, "core")
    ready_gate, ready_up = unpack(received, deep, wide)
    serve_router = finish(mine, other).reshape(pieces * deep, LANES)
    return (ready_gate[None], ready_up[None], serve_router)


def solution(mesh):
    placed = (P("owner", "rows", None), P("owner", "rows", None), P("rows", "owner"), P("rows"))
    return jax.shard_map(
        on_device,
        mesh=mesh,
        in_specs=placed,
        out_specs=(P(("owner", "rows"), None, None), P(("owner", "rows"), None, None), P()),
        check_vma=False,
    )
```

time: 103 us -> 101 us (0.981)
  Pallas kernels: 10.2 us -> 8.93 us
where the time goes in v3:
time: 101 us
  blocking collectives  86.3 us (85%)
  Pallas kernels  8.93 us (9%)
  starting transfers between devices  5.03 us (5%)
    all_to_all x1, blocking collectives, on_device(): lax.all_to_all(payload, 'rows', split_axis=0, concat_axis=0, tiled=True)  86.3 us
    ppermute x2, starting transfers between devices, swap(): return lax.ppermute(block, AXES, pairs)  5.03 us
    pallas_call x1, Pallas kernels, pack(): pl.pallas_call(pack_kernel, in_specs=[there, there], out_specs=WHOLE, out...  4.76 us
    pallas_call x1, Pallas kernels, unpack(): pl.pallas_call(unpack_kernel, in_specs=[WHOLE], out_specs=[there, there],...  2.94 us
  transfers between devices with their start and end apart: 2, of which 0 were waited for; matrix products, arithmetic and copies ran while one was open for 0% of the time, Pallas kernels for 8%

profile of v3, /device:TPU:1, one launch (start us, length us, event | category | flops | bytes accessed | tf_op | source)
XLA Modules:
  0.0 101.0 jit_solution(7187233326948488565)
XLA Ops:
  0.6 0.0 copy-start
  0.6 0.0 copy-start.1
  0.7 2.2 %collective-permute-start = (f32[32,64]{1,0:T(8,128)}, f32[32,64]{1,0:T(8,128)S(1)}, u32[]{:S(2)}, u32[]{:S(2)}) collective-permute-start(f32[32,64]{1,0:T(8,128)} %bitcast.5), channel_id=1, source_target_pairs={{0,64},{1,65},{2,66},{3,67},{4,68},{5,69},{6,70},{7,71},{8,72},{9,... | collective-permute-start | bytes 24584 | tf_op jit(solution)/shard_map/ppermute | solution.py:26
  2.8 4.8 %pack.1.payload_ref = bf16[32,800,128]{2,1,0:T(8,128)(2,1)S(1)} custom-call(f32[32,64,768]{2,1,0:T(8,128)} %gate_ref.1, f32[32,64,768]{2,1,0:T(8,128)} %up_ref.1), custom_call_target="tpu_custom_call" | custom-call | flops 100000000 | bytes 20000000 | tf_op jit(solution)/shard_map/pack/pallas_call | solution.py:56
  7.6 0.0 collective-permute-done.other_ref
  7.6 0.0 copy-done
  7.6 0.0 copy-done.1
  7.6 0.2 stamp.1
  7.8 86.3 %all_to_all.5.source = bf16[32,800,128]{2,1,0:T(8,128)(2,1)S(1)} all-to-all(bf16[32,800,128]{2,1,0:T(8,128)(2,1)S(1)} %stamp.1), channel_id=1, replica_groups=mesh['owner'=4,'rows'=32] {'rows'}, dimensions={0} | all-to-all | bytes 13107200 | tf_op jit(solution)/shard_map/all_to_all | solution.py:175
  94.2 2.8 %collective-permute-start.1 = (bf16[32,32,128]{2,1,0:T(8,128)(2,1)S(1)}, bf16[32,32,128]{2,1,0:T(8,128)(2,1)S(1)}, u32[]{:S(2)}, u32[]{:S(2)}) collective-permute-start(bf16[32,32,128]{2,1,0:T(8,128)(2,1)S(1)} %slice.4.mine_ref), channel_id=1, source_target_pairs={{0,32},{1,33},{2,34},{3,35},{4,36},{5,37},{6,38},{7,39},{8,40},{9,... | collective-permute-start | bytes 786440 | tf_op jit(solution)/shard_map/ppermute | solution.py:26
  97.0 2.9 %unpack.1 = (bf16[768,2048]{1,0:T(8,128)(2,1)}, bf16[768,2048]{1,0:T(8,128)(2,1)}) custom-call(bf16[32,800,128]{2,1,0:T(8,128)(2,1)S(1)} %all_to_all.5.source), custom_call_target="tpu_custom_call" | custom-call | flops 100000000 | bytes 20000000 | tf_op jit(solution)/shard_map/unpack/pallas_call | solution.py:127
  100.0 0.0 collective-permute-done.1.other_ref
  100.0 1.0 %finish.1 = bf16[32,64,128]{2,1,0:T(8,128)(2,1)} custom-call(bf16[32,32,128]{2,1,0:T(8,128)(2,1)S(1)} %slice.4.mine_ref, bf16[32,32,128]{2,1,0:T(8,128)(2,1)S(1)} %collective-permute-done.1.other_ref), custom_call_target="tpu_custom_call" | custom-call | tf_op jit(solution)/shard_map/finish/pallas_call | solution.py:158
  (1 shorter events, 0.0 us)
Async XLA Ops:
  0.6 7.0 %copy-start = (f32[64,32]{0,1:T(8,128)S(1)}, f32[64,32]{0,1:T(8,128)}, u32[]{:S(2)}) copy-start(f32[64,32]{0,1:T(8,128)} %param.6) | copy-start | bytes 24580
  0.6 7.0 %copy-start.1 = (f32[64]{0:T(128)S(1)}, f32[64]{0:T(128)}, u32[]{:S(2)}) copy-start(f32[64]{0:T(128)} %param.7) | copy-start | bytes 772
  0.7 7.0 %collective-permute-start = (f32[32,64]{1,0:T(8,128)}, f32[32,64]{1,0:T(8,128)S(1)}, u32[]{:S(2)}, u32[]{:S(2)}) collective-permute-start(f32[32,64]{1,0:T(8,128)} %bitcast.5), channel_id=1, source_target_pairs={{0,64},{1,65},{2,66},{3,67},{4,68},{5,69},{6,70},{7,71},{8,72},{9,... | collective-permute-start | bytes 24584 | tf_op jit(solution)/shard_map/ppermute | solution.py:26
  94.2 5.8 %collective-permute-start.1 = (bf16[32,32,128]{2,1,0:T(8,128)(2,1)S(1)}, bf16[32,32,128]{2,1,0:T(8,128)(2,1)S(1)}, u32[]{:S(2)}, u32[]{:S(2)}) collective-permute-start(bf16[32,32,128]{2,1,0:T(8,128)(2,1)S(1)} %slice.4.mine_ref), channel_id=1, source_target_pairs={{0,32},{1,33},{2,34},{3,35},{4,36},{5,37},{6,38},{7,39},{8,40},{9,... | collective-permute-start | bytes 786440 | tf_op jit(solution)/shard_map/ppermute | solution.py:26

commit v4 on v3

--- a/solution.py
+++ b/solution.py
@@ -7,6 +7,8 @@
 
 AXES = ("owner", "rows")
 LANES = 128
+MEMBERS = [(3 - z) * 8 + (1 - yh) * 4 + (3 - x) for z in range(4) for yh in range(2) for x in range(4)]
+SLOT = [MEMBERS.index(row) for row in range(32)]
 WHOLE = pl.BlockSpec(memory_space=pltpu.VMEM)
 COST = pl.CostEstimate(flops=100_000_000, bytes_accessed=20_000_000, transcendentals=0)
 
@@ -38,14 +40,17 @@
         for which in range(2):
             copy(which, batch).start()
 
-    @pl.loop(0, batches)
-    def _(batch):
+    for batch in range(batches):
         for which in range(2):
             copy(which, batch).wait()
-            for tile in range(tiles):
-                out_ref[pl.ds(batch * step, step), pl.ds((which * tiles + tile) * deep, deep), :] = held[
-                    which, batch, :, :, tile * LANES : (tile + 1) * LANES
-                ].astype(jnp.bfloat16)
+            for piece in range(step):
+                slot = SLOT[batch * step + piece]
+
+                @pl.loop(0, tiles)
+                def _(tile):
+                    first = pl.multiple_of((which * tiles + tile) * deep, deep)
+                    lanes = pl.ds(pl.multiple_of(tile * LANES, LANES), LANES)
+                    out_ref[slot, pl.ds(first, deep), :] = held[which, batch, piece, :, lanes].astype(jnp.bfloat16)
 
 
 def pack(gate, up, extra):
@@ -110,8 +115,8 @@
         for which in range(2):
             start = pl.multiple_of((which * tiles + tile) * deep, deep)
             for i in range(pieces // pair):
-                block = source[pl.ds(i * pair, pair), pl.ds(start, deep), :]
-                held[which, tile, :, i * LANES : (i + 1) * LANES] = block.reshape(LANES, LANES).T
+                parts = [source[SLOT[i * pair + part], pl.ds(start, deep), :] for part in range(pair)]
+                held[which, tile, :, i * LANES : (i + 1) * LANES] = jnp.concatenate(parts, axis=0).T
             copy(which, tile).start()
 
     @pl.loop(0, tiles)
@@ -150,7 +155,9 @@
     crossed = jnp.where(own, other, mine)
     crossed = jnp.where(odd == 1, pltpu.roll(crossed, quarter, 1), pltpu.roll(crossed, lanes - quarter, 1))
     for h, block in enumerate((jnp.where(own, mine, other), crossed)):
-        out_ref[:, h * half : (h + 1) * half, :] = block.astype(jnp.bfloat16).reshape(pieces, half, lanes)
+        block = block.astype(jnp.bfloat16).reshape(pieces, half, lanes)
+        for row in range(pieces):
+            out_ref[row, h * half : (h + 1) * half, :] = block[SLOT[row]]
 
 
 def finish(mine, other):
@@ -172,7 +179,9 @@
     payload = pack(train_gate, train_up, deep // 2)
     body = payload.shape[1] - deep // 2
     payload = stamp(payload, part, other_part, router_gain[None, :])
-    received = lax.all_to_all(payload, "rows", split_axis=0, concat_axis=0, tiled=True)
+    received = lax.all_to_all(
+        payload, "rows", split_axis=0, concat_axis=0, axis_index_groups=[MEMBERS], tiled=True
+    )
     mine = received[:, body:, :]
     other = swap(mine, "core")
     ready_gate, ready_up = unpack(received, deep, wide)

time: 101 us -> 97 us (0.960)
  blocking collectives: 86.3 us -> 82.8 us
    all_to_all x1, blocking collectives: 86.3 us -> 82.8 us  [on_device(): lax.all_to_all(payload, 'rows', split_axis=0, concat_axis=0, axis_index_g...]
where the time goes in v4:
time: 97 us; the launch traced here: 96.9 us
  blocking collectives  82.8 us (85%)
  Pallas kernels  9.06 us (9%)
  starting transfers between devices  4.32 us (4%)
    all_to_all x1, blocking collectives, on_device(): lax.all_to_all(payload, 'rows', split_axis=0, concat_axis=0, axis_index_g...  82.8 us
    pallas_call x1, Pallas kernels, pack(): pl.pallas_call(pack_kernel, in_specs=[there, there], out_specs=WHOLE, out...  4.89 us
    ppermute x2, starting transfers between devices, swap(): return lax.ppermute(block, AXES, pairs)  4.32 us
    pallas_call x1, Pallas kernels, unpack(): pl.pallas_call(unpack_kernel, in_specs=[WHOLE], out_specs=[there, there],...  2.94 us
  transfers between devices with their start and end apart: 2, of which 0 were waited for; matrix products, arithmetic and copies ran while one was open for 0% of the time, Pallas kernels for 8%

profile of v4, /device:TPU:1, one launch (start us, length us, event | category | flops | bytes accessed | tf_op | source)
XLA Modules:
  0.0 96.9 jit_solution(14922351354521364204)
XLA Ops:
  0.6 0.0 copy-start
  0.6 0.0 copy-start.1
  0.7 2.2 %collective-permute-start = (f32[32,64]{1,0:T(8,128)}, f32[32,64]{1,0:T(8,128)S(1)}, u32[]{:S(2)}, u32[]{:S(2)}) collective-permute-start(f32[32,64]{1,0:T(8,128)} %bitcast.5), channel_id=1, source_target_pairs={{0,64},{1,65},{2,66},{3,67},{4,68},{5,69},{6,70},{7,71},{8,72},{9,... | collective-permute-start | bytes 24584 | tf_op jit(solution)/shard_map/ppermute | solution.py:28
  2.8 4.9 %pack.1.payload_ref = bf16[32,800,128]{2,1,0:T(8,128)(2,1)S(1)} custom-call(f32[32,64,768]{2,1,0:T(8,128)} %gate_ref.1, f32[32,64,768]{2,1,0:T(8,128)} %up_ref.1), custom_call_target="tpu_custom_call" | custom-call | flops 100000000 | bytes 20000000 | tf_op jit(solution)/shard_map/pack/pallas_call | solution.py:61
  7.7 0.0 collective-permute-done.other_ref
  7.8 0.0 copy-done
  7.8 0.0 copy-done.1
  7.8 0.2 stamp.1
  8.0 82.8 %all_to_all.5.source = bf16[32,800,128]{2,1,0:T(8,128)(2,1)S(1)} all-to-all(bf16[32,800,128]{2,1,0:T(8,128)(2,1)S(1)} %stamp.1), channel_id=1, replica_groups={{31,30,29,28,27,26,25,24,23,22,21,20,19,18,17,16,15,14,13,12,11,10,9,8,..., dimensions={0} | all-to-all | bytes 13107200 | tf_op jit(solution)/shard_map/all_to_all | solution.py:182
  90.8 2.1 %collective-permute-start.1 = (bf16[32,32,128]{2,1,0:T(8,128)(2,1)S(1)}, bf16[32,32,128]{2,1,0:T(8,128)(2,1)S(1)}, u32[]{:S(2)}, u32[]{:S(2)}) collective-permute-start(bf16[32,32,128]{2,1,0:T(8,128)(2,1)S(1)} %slice.4.mine_ref), channel_id=1, source_target_pairs={{0,32},{1,33},{2,34},{3,35},{4,36},{5,37},{6,38},{7,39},{8,40},{9,... | collective-permute-start | bytes 786440 | tf_op jit(solution)/shard_map/ppermute | solution.py:28
  92.9 2.9 %unpack.1 = (bf16[768,2048]{1,0:T(8,128)(2,1)}, bf16[768,2048]{1,0:T(8,128)(2,1)}) custom-call(bf16[32,800,128]{2,1,0:T(8,128)(2,1)S(1)} %all_to_all.5.source), custom_call_target="tpu_custom_call" | custom-call | flops 100000000 | bytes 20000000 | tf_op jit(solution)/shard_map/unpack/pallas_call | solution.py:132
  95.8 0.0 collective-permute-done.1.other_ref
  95.8 1.0 %finish.1 = bf16[32,64,128]{2,1,0:T(8,128)(2,1)} custom-call(bf16[32,32,128]{2,1,0:T(8,128)(2,1)S(1)} %slice.4.mine_ref, bf16[32,32,128]{2,1,0:T(8,128)(2,1)S(1)} %collective-permute-done.1.other_ref), custom_call_target="tpu_custom_call" | custom-call | tf_op jit(solution)/shard_map/finish/pallas_call | solution.py:165
  (1 shorter events, 0.0 us)
Async XLA Ops:
  0.6 7.1 %copy-start = (f32[64,32]{0,1:T(8,128)S(1)}, f32[64,32]{0,1:T(8,128)}, u32[]{:S(2)}) copy-start(f32[64,32]{0,1:T(8,128)} %param.6) | copy-start | bytes 24580
  0.6 7.1 %copy-start.1 = (f32[64]{0:T(128)S(1)}, f32[64]{0:T(128)}, u32[]{:S(2)}) copy-start(f32[64]{0:T(128)} %param.7) | copy-start | bytes 772
  0.7 7.1 %collective-permute-start = (f32[32,64]{1,0:T(8,128)}, f32[32,64]{1,0:T(8,128)S(1)}, u32[]{:S(2)}, u32[]{:S(2)}) collective-permute-start(f32[32,64]{1,0:T(8,128)} %bitcast.5), channel_id=1, source_target_pairs={{0,64},{1,65},{2,66},{3,67},{4,68},{5,69},{6,70},{7,71},{8,72},{9,... | collective-permute-start | bytes 24584 | tf_op jit(solution)/shard_map/ppermute | solution.py:28
  90.8 5.1 %collective-permute-start.1 = (bf16[32,32,128]{2,1,0:T(8,128)(2,1)S(1)}, bf16[32,32,128]{2,1,0:T(8,128)(2,1)S(1)}, u32[]{:S(2)}, u32[]{:S(2)}) collective-permute-start(bf16[32,32,128]{2,1,0:T(8,128)(2,1)S(1)} %slice.4.mine_ref), channel_id=1, source_target_pairs={{0,32},{1,33},{2,34},{3,35},{4,36},{5,37},{6,38},{7,39},{8,40},{9,... | collective-permute-start | bytes 786440 | tf_op jit(solution)/shard_map/ppermute | solution.py:28

commit v5 on v4

--- a/solution.py
+++ b/solution.py
@@ -7,7 +7,7 @@
 
 AXES = ("owner", "rows")
 LANES = 128
-MEMBERS = [(3 - z) * 8 + (1 - yh) * 4 + (3 - x) for z in range(4) for yh in range(2) for x in range(4)]
+MEMBERS = [z * 8 + yh * 4 + x for z in (2, 3, 0, 1) for yh in (1, 0) for x in (3, 2, 1, 0)]
 SLOT = [MEMBERS.index(row) for row in range(32)]
 WHOLE = pl.BlockSpec(memory_space=pltpu.VMEM)
 COST = pl.CostEstimate(flops=100_000_000, bytes_accessed=20_000_000, transcendentals=0)
@@ -45,17 +45,16 @@
             copy(which, batch).wait()
             for piece in range(step):
                 slot = SLOT[batch * step + piece]
-
-                @pl.loop(0, tiles)
-                def _(tile):
-                    first = pl.multiple_of((which * tiles + tile) * deep, deep)
-                    lanes = pl.ds(pl.multiple_of(tile * LANES, LANES), LANES)
-                    out_ref[slot, pl.ds(first, deep), :] = held[which, batch, piece, :, lanes].astype(jnp.bfloat16)
+                for tile in range(tiles):
+                    first = (which * tiles + tile) * deep
+                    out_ref[slot, first : first + deep, :] = held[
+                        which, batch, piece, :, tile * LANES : (tile + 1) * LANES
+                    ].astype(jnp.bfloat16)
 
 
 def pack(gate, up, extra):
     pieces, deep, wide = gate.shape
-    step = 4
+    step = 8
     total = 2 * deep * wide // LANES + extra
     there = pl.BlockSpec(memory_space=pltpu.HBM)
     return pl.pallas_call(
@@ -144,20 +143,31 @@
     )(received)
 
 
-def finish_kernel(mine_ref, other_ref, out_ref):
+def finish_kernel(mine_ref, other_ref, out_ref, held, sems):
     pieces, half, lanes = mine_ref.shape
+    parts = sems.shape[0]
+    step = pieces // parts
     upper = lax.axis_index("owner") % 2
-    mine = mine_ref[...].reshape(pieces * half, lanes).astype(jnp.float32)
-    other = other_ref[...].reshape(pieces * half, lanes).astype(jnp.float32)
     quarter = lanes // 4
-    odd = lax.broadcasted_iota(jnp.int32, mine.shape, 1) // quarter % 2
+    odd = lax.broadcasted_iota(jnp.int32, (step * half, lanes), 1) // quarter % 2
     own = odd == upper
-    crossed = jnp.where(own, other, mine)
-    crossed = jnp.where(odd == 1, pltpu.roll(crossed, quarter, 1), pltpu.roll(crossed, lanes - quarter, 1))
-    for h, block in enumerate((jnp.where(own, mine, other), crossed)):
-        block = block.astype(jnp.bfloat16).reshape(pieces, half, lanes)
-        for row in range(pieces):
-            out_ref[row, h * half : (h + 1) * half, :] = block[SLOT[row]]
+
+    def copy(part):
+        rows = pl.ds(min(MEMBERS[part * step : (part + 1) * step]), step)
+        return pltpu.make_async_copy(held.at[rows], out_ref.at[rows], sems.at[part])
+
+    for part in range(parts):
+        mine = mine_ref[part * step : (part + 1) * step].reshape(step * half, lanes).astype(jnp.float32)
+        other = other_ref[part * step : (part + 1) * step].reshape(step * half, lanes).astype(jnp.float32)
+        crossed = jnp.where(own, other, mine)
+        crossed = jnp.where(odd == 1, pltpu.roll(crossed, quarter, 1), pltpu.roll(crossed, lanes - quarter, 1))
+        for h, block in enumerate((jnp.where(own, mine, other), crossed)):
+            block = block.astype(jnp.bfloat16).reshape(step, half, lanes)
+            for piece in range(step):
+                held[MEMBERS[part * step + piece], h * half : (h + 1) * half, :] = block[piece]
+        copy(part).start()
+    for part in range(parts):
+        copy(part).wait()
 
 
 def finish(mine, other):
@@ -165,8 +175,9 @@
     return pl.pallas_call(
         finish_kernel,
         in_specs=[WHOLE, WHOLE],
-        out_specs=WHOLE,
+        out_specs=pl.BlockSpec(memory_space=pltpu.HBM),
         out_shape=jax.ShapeDtypeStruct((pieces, 2 * half, lanes), jnp.bfloat16),
+        scratch_shapes=[pltpu.VMEM((pieces, 2 * half, lanes), jnp.bfloat16), pltpu.SemaphoreType.DMA((4,))],
         compiler_params=pltpu.CompilerParams(vmem_limit_bytes=8 * 1024 * 1024),
         name="finish",
     )(mine, other)

time: 97 us -> 96.5 us (level)
  no operation moved by 1% of the time
where the time goes in v5:
time: 96.5 us; the launch traced here: 96.4 us
  blocking collectives  82.1 us (85%)
  Pallas kernels  8.86 us (9%)
  starting transfers between devices  4.63 us (5%)
    all_to_all x1, blocking collectives, on_device(): lax.all_to_all(payload, 'rows', split_axis=0, concat_axis=0, axis_index_g...  82.1 us
    pallas_call x1, Pallas kernels, pack(): pl.pallas_call(pack_kernel, in_specs=[there, there], out_specs=WHOLE, out...  4.78 us
    ppermute x2, starting transfers between devices, swap(): return lax.ppermute(block, AXES, pairs)  4.63 us
    pallas_call x1, Pallas kernels, unpack(): pl.pallas_call(unpack_kernel, in_specs=[WHOLE], out_specs=[there, there],...  2.94 us
  transfers between devices with their start and end apart: 2, of which 0 were waited for; matrix products, arithmetic and copies ran while one was open for 0% of the time, Pallas kernels for 8%

profile of v5, /device:TPU:1, one launch (start us, length us, event | category | flops | bytes accessed | tf_op | source)
XLA Modules:
  0.0 96.4 jit_solution(4600958405628977369)
XLA Ops:
  0.6 0.0 copy-start
  0.6 0.0 copy-start.1
  0.7 2.2 %collective-permute-start = (f32[32,64]{1,0:T(8,128)}, f32[32,64]{1,0:T(8,128)S(1)}, u32[]{:S(2)}, u32[]{:S(2)}) collective-permute-start(f32[32,64]{1,0:T(8,128)} %bitcast.5), channel_id=1, source_target_pairs={{0,64},{1,65},{2,66},{3,67},{4,68},{5,69},{6,70},{7,71},{8,72},{9,... | collective-permute-start | bytes 24584 | tf_op jit(solution)/shard_map/ppermute | solution.py:28
  2.8 4.8 %pack.1.payload_ref = bf16[32,800,128]{2,1,0:T(8,128)(2,1)S(1)} custom-call(f32[32,64,768]{2,1,0:T(8,128)} %gate_ref.1, f32[32,64,768]{2,1,0:T(8,128)} %up_ref.1), custom_call_target="tpu_custom_call" | custom-call | flops 100000000 | bytes 20000000 | tf_op jit(solution)/shard_map/pack/pallas_call | solution.py:60
  7.6 0.0 collective-permute-done.other_ref
  7.6 0.0 copy-done
  7.6 0.0 copy-done.1
  7.7 0.2 stamp.1
  7.9 82.1 %all_to_all.5.source = bf16[32,800,128]{2,1,0:T(8,128)(2,1)S(1)} all-to-all(bf16[32,800,128]{2,1,0:T(8,128)(2,1)S(1)} %stamp.1), channel_id=1, replica_groups={{23,22,21,20,19,18,17,16,31,30,29,28,27,26,25,24,7,6,5,4,3,2,1,0,15,14,..., dimensions={0} | all-to-all | bytes 13107200 | tf_op jit(solution)/shard_map/all_to_all | solution.py:193
  90.0 2.4 %collective-permute-start.1 = (bf16[32,32,128]{2,1,0:T(8,128)(2,1)S(1)}, bf16[32,32,128]{2,1,0:T(8,128)(2,1)S(1)}, u32[]{:S(2)}, u32[]{:S(2)}) collective-permute-start(bf16[32,32,128]{2,1,0:T(8,128)(2,1)S(1)} %slice.4.mine_ref), channel_id=1, source_target_pairs={{0,32},{1,33},{2,34},{3,35},{4,36},{5,37},{6,38},{7,39},{8,40},{9,... | collective-permute-start | bytes 786440 | tf_op jit(solution)/shard_map/ppermute | solution.py:28
  92.4 2.9 %unpack.1 = (bf16[768,2048]{1,0:T(8,128)(2,1)}, bf16[768,2048]{1,0:T(8,128)(2,1)}) custom-call(bf16[32,800,128]{2,1,0:T(8,128)(2,1)S(1)} %all_to_all.5.source), custom_call_target="tpu_custom_call" | custom-call | flops 100000000 | bytes 20000000 | tf_op jit(solution)/shard_map/unpack/pallas_call | solution.py:131
  95.4 0.0 collective-permute-done.1.other_ref
  95.4 1.0 finish.1
  (1 shorter events, 0.0 us)
Async XLA Ops:
  0.6 7.0 %copy-start = (f32[64,32]{0,1:T(8,128)S(1)}, f32[64,32]{0,1:T(8,128)}, u32[]{:S(2)}) copy-start(f32[64,32]{0,1:T(8,128)} %param.6) | copy-start | bytes 24580
  0.6 7.0 %copy-start.1 = (f32[64]{0:T(128)S(1)}, f32[64]{0:T(128)}, u32[]{:S(2)}) copy-start(f32[64]{0:T(128)} %param.7) | copy-start | bytes 772
  0.7 7.0 %collective-permute-start = (f32[32,64]{1,0:T(8,128)}, f32[32,64]{1,0:T(8,128)S(1)}, u32[]{:S(2)}, u32[]{:S(2)}) collective-permute-start(f32[32,64]{1,0:T(8,128)} %bitcast.5), channel_id=1, source_target_pairs={{0,64},{1,65},{2,66},{3,67},{4,68},{5,69},{6,70},{7,71},{8,72},{9,... | collective-permute-start | bytes 24584 | tf_op jit(solution)/shard_map/ppermute | solution.py:28
  90.0 5.4 %collective-permute-start.1 = (bf16[32,32,128]{2,1,0:T(8,128)(2,1)S(1)}, bf16[32,32,128]{2,1,0:T(8,128)(2,1)S(1)}, u32[]{:S(2)}, u32[]{:S(2)}) collective-permute-start(bf16[32,32,128]{2,1,0:T(8,128)(2,1)S(1)} %slice.4.mine_ref), channel_id=1, source_target_pairs={{0,32},{1,33},{2,34},{3,35},{4,36},{5,37},{6,38},{7,39},{8,40},{9,... | collective-permute-start | bytes 786440 | tf_op jit(solution)/shard_map/ppermute | solution.py:28

commit v6 on v5

--- a/solution.py
+++ b/solution.py
@@ -7,7 +7,7 @@
 
 AXES = ("owner", "rows")
 LANES = 128
-MEMBERS = [z * 8 + yh * 4 + x for z in (2, 3, 0, 1) for yh in (1, 0) for x in (3, 2, 1, 0)]
+MEMBERS = [z * 8 + yh * 4 + x for z in (2, 3, 0, 1) for yh in (1, 0) for x in (2, 3, 0, 1)]
 SLOT = [MEMBERS.index(row) for row in range(32)]
 WHOLE = pl.BlockSpec(memory_space=pltpu.VMEM)
 COST = pl.CostEstimate(flops=100_000_000, bytes_accessed=20_000_000, transcendentals=0)

time: 96.5 us -> 96 us (level)
  no operation moved by 1% of the time
where the time goes in v6:
time: 96 us; the launch traced here: 95.8 us
  blocking collectives  81.8 us (85%)
  Pallas kernels  8.86 us (9%)
  starting transfers between devices  4.33 us (5%)
    all_to_all x1, blocking collectives, on_device(): lax.all_to_all(payload, 'rows', split_axis=0, concat_axis=0, axis_index_g...  81.8 us
    pallas_call x1, Pallas kernels, pack(): pl.pallas_call(pack_kernel, in_specs=[there, there], out_specs=WHOLE, out...  4.78 us
    ppermute x2, starting transfers between devices, swap(): return lax.ppermute(block, AXES, pairs)  4.33 us
    pallas_call x1, Pallas kernels, unpack(): pl.pallas_call(unpack_kernel, in_specs=[WHOLE], out_specs=[there, there],...  2.94 us
  transfers between devices with their start and end apart: 2, of which 0 were waited for; matrix products, arithmetic and copies ran while one was open for 0% of the time, Pallas kernels for 8%

profile of v6, /device:TPU:1, one launch (start us, length us, event | category | flops | bytes accessed | tf_op | source)
XLA Modules:
  0.0 95.8 jit_solution(3990986933388317904)
XLA Ops:
  0.6 0.0 copy-start
  0.6 0.0 copy-start.1
  0.7 2.2 %collective-permute-start = (f32[32,64]{1,0:T(8,128)}, f32[32,64]{1,0:T(8,128)S(1)}, u32[]{:S(2)}, u32[]{:S(2)}) collective-permute-start(f32[32,64]{1,0:T(8,128)} %bitcast.5), channel_id=1, source_target_pairs={{0,64},{1,65},{2,66},{3,67},{4,68},{5,69},{6,70},{7,71},{8,72},{9,... | collective-permute-start | bytes 24584 | tf_op jit(solution)/shard_map/ppermute | solution.py:28
  2.8 4.8 %pack.1.payload_ref = bf16[32,800,128]{2,1,0:T(8,128)(2,1)S(1)} custom-call(f32[32,64,768]{2,1,0:T(8,128)} %gate_ref.1, f32[32,64,768]{2,1,0:T(8,128)} %up_ref.1), custom_call_target="tpu_custom_call" | custom-call | flops 100000000 | bytes 20000000 | tf_op jit(solution)/shard_map/pack/pallas_call | solution.py:60
  7.6 0.0 collective-permute-done.other_ref
  7.6 0.0 copy-done
  7.6 0.0 copy-done.1
  7.7 0.2 stamp.1
  7.9 81.8 %all_to_all.5.source = bf16[32,800,128]{2,1,0:T(8,128)(2,1)S(1)} all-to-all(bf16[32,800,128]{2,1,0:T(8,128)(2,1)S(1)} %stamp.1), channel_id=1, replica_groups={{22,23,20,21,18,19,16,17,30,31,28,29,26,27,24,25,6,7,4,5,2,3,0,1,14,15,..., dimensions={0} | all-to-all | bytes 13107200 | tf_op jit(solution)/shard_map/all_to_all | solution.py:193
  89.7 2.1 %collective-permute-start.1 = (bf16[32,32,128]{2,1,0:T(8,128)(2,1)S(1)}, bf16[32,32,128]{2,1,0:T(8,128)(2,1)S(1)}, u32[]{:S(2)}, u32[]{:S(2)}) collective-permute-start(bf16[32,32,128]{2,1,0:T(8,128)(2,1)S(1)} %slice.4.mine_ref), channel_id=1, source_target_pairs={{0,32},{1,33},{2,34},{3,35},{4,36},{5,37},{6,38},{7,39},{8,40},{9,... | collective-permute-start | bytes 786440 | tf_op jit(solution)/shard_map/ppermute | solution.py:28
  91.9 2.9 %unpack.1 = (bf16[768,2048]{1,0:T(8,128)(2,1)}, bf16[768,2048]{1,0:T(8,128)(2,1)}) custom-call(bf16[32,800,128]{2,1,0:T(8,128)(2,1)S(1)} %all_to_all.5.source), custom_call_target="tpu_custom_call" | custom-call | flops 100000000 | bytes 20000000 | tf_op jit(solution)/shard_map/unpack/pallas_call | solution.py:131
  94.8 0.0 collective-permute-done.1.other_ref
  94.8 1.0 %finish.1 = bf16[32,64,128]{2,1,0:T(8,128)(2,1)} custom-call(bf16[32,32,128]{2,1,0:T(8,128)(2,1)S(1)} %slice.4.mine_ref, bf16[32,32,128]{2,1,0:T(8,128)(2,1)S(1)} %collective-permute-done.1.other_ref), custom_call_target="tpu_custom_call" | custom-call | tf_op jit(solution)/shard_map/finish/pallas_call | solution.py:175
  (1 shorter events, 0.0 us)
Async XLA Ops:
  0.6 7.0 %copy-start = (f32[64,32]{0,1:T(8,128)S(1)}, f32[64,32]{0,1:T(8,128)}, u32[]{:S(2)}) copy-start(f32[64,32]{0,1:T(8,128)} %param.6) | copy-start | bytes 24580
  0.6 7.0 %copy-start.1 = (f32[64]{0:T(128)S(1)}, f32[64]{0:T(128)}, u32[]{:S(2)}) copy-start(f32[64]{0:T(128)} %param.7) | copy-start | bytes 772
  0.7 7.0 %collective-permute-start = (f32[32,64]{1,0:T(8,128)}, f32[32,64]{1,0:T(8,128)S(1)}, u32[]{:S(2)}, u32[]{:S(2)}) collective-permute-start(f32[32,64]{1,0:T(8,128)} %bitcast.5), channel_id=1, source_target_pairs={{0,64},{1,65},{2,66},{3,67},{4,68},{5,69},{6,70},{7,71},{8,72},{9,... | collective-permute-start | bytes 24584 | tf_op jit(solution)/shard_map/ppermute | solution.py:28
  89.7 5.1 %collective-permute-start.1 = (bf16[32,32,128]{2,1,0:T(8,128)(2,1)S(1)}, bf16[32,32,128]{2,1,0:T(8,128)(2,1)S(1)}, u32[]{:S(2)}, u32[]{:S(2)}) collective-permute-start(bf16[32,32,128]{2,1,0:T(8,128)(2,1)S(1)} %slice.4.mine_ref), channel_id=1, source_target_pairs={{0,32},{1,33},{2,34},{3,35},{4,36},{5,37},{6,38},{7,39},{8,40},{9,... | collective-permute-start | bytes 786440 | tf_op jit(solution)/shard_map/ppermute | solution.py:28

commit v7 on v6

--- a/solution.py
+++ b/solution.py
@@ -105,9 +105,12 @@
     tiles = held.shape[1]
     pair = LANES // deep
 
-    def copy(which, tile):
-        out = (gate_ref, up_ref)[which]
-        return pltpu.make_async_copy(held.at[which, tile], out.at[pl.ds(tile * LANES, LANES)], sems.at[which, tile])
+    groups = pieces // pair
+    width = groups // 2 * LANES
+
+    def copy(which, tile, half):
+        out = (gate_ref, up_ref)[which].at[pl.ds(tile * LANES, LANES), pl.ds(half * width, width)]
+        return pltpu.make_async_copy(held.at[which, tile, :, pl.ds(half * width, width)], out, sems.at[which, tile, half])
 
     @pl.loop(0, tiles)
     def _(tile):
@@ -116,12 +119,14 @@
             for i in range(pieces // pair):
                 parts = [source[SLOT[i * pair + part], pl.ds(start, deep), :] for part in range(pair)]
                 held[which, tile, :, i * LANES : (i + 1) * LANES] = jnp.concatenate(parts, axis=0).T
-            copy(which, tile).start()
+                if i % (groups // 2) == groups // 2 - 1:
+                    copy(which, tile, i // (groups // 2)).start()
 
     @pl.loop(0, tiles)
     def _(tile):
         for which in range(2):
-            copy(which, tile).wait()
+            for half in range(2):
+                copy(which, tile, half).wait()
 
 
 def unpack(received, deep, wide):
@@ -135,7 +140,7 @@
         out_shape=[shape, shape],
         scratch_shapes=[
             pltpu.VMEM((2, wide // LANES, LANES, pieces * deep), jnp.bfloat16),
-            pltpu.SemaphoreType.DMA((2, wide // LANES)),
+            pltpu.SemaphoreType.DMA((2, wide // LANES, 2)),
         ],
         compiler_params=pltpu.CompilerParams(vmem_limit_bytes=24 * 1024 * 1024),
         cost_estimate=COST,

time: 96 us -> 96.1 us (level)
  no operation moved by 1% of the time
where the time goes in v7:
time: 96.1 us; the launch traced here: 95.8 us
  blocking collectives  81.8 us (85%)
  Pallas kernels  8.88 us (9%)
  starting transfers between devices  4.33 us (5%)
    all_to_all x1, blocking collectives, on_device(): lax.all_to_all(payload, 'rows', split_axis=0, concat_axis=0, axis_index_g...  81.8 us
    pallas_call x1, Pallas kernels, pack(): pl.pallas_call(pack_kernel, in_specs=[there, there], out_specs=WHOLE, out...  4.78 us
    ppermute x2, starting transfers between devices, swap(): return lax.ppermute(block, AXES, pairs)  4.33 us
    pallas_call x1, Pallas kernels, unpack(): pl.pallas_call(unpack_kernel, in_specs=[WHOLE], out_specs=[there, there],...  2.96 us
  transfers between devices with their start and end apart: 2, of which 0 were waited for; matrix products, arithmetic and copies ran while one was open for 0% of the time, Pallas kernels for 8%

profile of v7, /device:TPU:1, one launch (start us, length us, event | category | flops | bytes accessed | tf_op | source)
XLA Modules:
  0.0 95.8 jit_solution(9240535419697593915)
XLA Ops:
  0.6 0.0 copy-start
  0.6 0.0 copy-start.1
  0.7 2.2 %collective-permute-start = (f32[32,64]{1,0:T(8,128)}, f32[32,64]{1,0:T(8,128)S(1)}, u32[]{:S(2)}, u32[]{:S(2)}) collective-permute-start(f32[32,64]{1,0:T(8,128)} %bitcast.5), channel_id=1, source_target_pairs={{0,64},{1,65},{2,66},{3,67},{4,68},{5,69},{6,70},{7,71},{8,72},{9,... | collective-permute-start | bytes 24584 | tf_op jit(solution)/shard_map/ppermute | solution.py:28
  2.8 4.8 %pack.1.payload_ref = bf16[32,800,128]{2,1,0:T(8,128)(2,1)S(1)} custom-call(f32[32,64,768]{2,1,0:T(8,128)} %gate_ref.1, f32[32,64,768]{2,1,0:T(8,128)} %up_ref.1), custom_call_target="tpu_custom_call" | custom-call | flops 100000000 | bytes 20000000 | tf_op jit(solution)/shard_map/pack/pallas_call | solution.py:60
  7.6 0.0 collective-permute-done.other_ref
  7.6 0.0 copy-done
  7.6 0.0 copy-done.1
  7.7 0.2 stamp.1
  7.9 81.8 %all_to_all.5.source = bf16[32,800,128]{2,1,0:T(8,128)(2,1)S(1)} all-to-all(bf16[32,800,128]{2,1,0:T(8,128)(2,1)S(1)} %stamp.1), channel_id=1, replica_groups={{22,23,20,21,18,19,16,17,30,31,28,29,26,27,24,25,6,7,4,5,2,3,0,1,14,15,..., dimensions={0} | all-to-all | bytes 13107200 | tf_op jit(solution)/shard_map/all_to_all | solution.py:198
  89.7 2.1 %collective-permute-start.1 = (bf16[32,32,128]{2,1,0:T(8,128)(2,1)S(1)}, bf16[32,32,128]{2,1,0:T(8,128)(2,1)S(1)}, u32[]{:S(2)}, u32[]{:S(2)}) collective-permute-start(bf16[32,32,128]{2,1,0:T(8,128)(2,1)S(1)} %slice.4.mine_ref), channel_id=1, source_target_pairs={{0,32},{1,33},{2,34},{3,35},{4,36},{5,37},{6,38},{7,39},{8,40},{9,... | collective-permute-start | bytes 786440 | tf_op jit(solution)/shard_map/ppermute | solution.py:28
  91.9 3.0 %unpack.1 = (bf16[768,2048]{1,0:T(8,128)(2,1)}, bf16[768,2048]{1,0:T(8,128)(2,1)}) custom-call(bf16[32,800,128]{2,1,0:T(8,128)(2,1)S(1)} %all_to_all.5.source), custom_call_target="tpu_custom_call" | custom-call | flops 100000000 | bytes 20000000 | tf_op jit(solution)/shard_map/unpack/pallas_call | solution.py:136
  94.8 0.0 collective-permute-done.1.other_ref
  94.8 1.0 finish.1
  (1 shorter events, 0.0 us)
Async XLA Ops:
  0.6 7.0 %copy-start = (f32[64,32]{0,1:T(8,128)S(1)}, f32[64,32]{0,1:T(8,128)}, u32[]{:S(2)}) copy-start(f32[64,32]{0,1:T(8,128)} %param.6) | copy-start | bytes 24580
  0.6 7.0 %copy-start.1 = (f32[64]{0:T(128)S(1)}, f32[64]{0:T(128)}, u32[]{:S(2)}) copy-start(f32[64]{0:T(128)} %param.7) | copy-start | bytes 772
  0.7 7.0 %collective-permute-start = (f32[32,64]{1,0:T(8,128)}, f32[32,64]{1,0:T(8,128)S(1)}, u32[]{:S(2)}, u32[]{:S(2)}) collective-permute-start(f32[32,64]{1,0:T(8,128)} %bitcast.5), channel_id=1, source_target_pairs={{0,64},{1,65},{2,66},{3,67},{4,68},{5,69},{6,70},{7,71},{8,72},{9,... | collective-permute-start | bytes 24584 | tf_op jit(solution)/shard_map/ppermute | solution.py:28
  89.7 5.1 %collective-permute-start.1 = (bf16[32,32,128]{2,1,0:T(8,128)(2,1)S(1)}, bf16[32,32,128]{2,1,0:T(8,128)(2,1)S(1)}, u32[]{:S(2)}, u32[]{:S(2)}) collective-permute-start(bf16[32,32,128]{2,1,0:T(8,128)(2,1)S(1)} %slice.4.mine_ref), channel_id=1, source_target_pairs={{0,32},{1,33},{2,34},{3,35},{4,36},{5,37},{6,38},{7,39},{8,40},{9,... | collective-permute-start | bytes 786440 | tf_op jit(solution)/shard_map/ppermute | solution.py:28
